TPU v7x, 32 devices: a whole 2x2x4 slice. The times are simulated.
32 devices in a mesh: dp: 4 (over x, core), section: 2 (over y), tensor: 4 (over z).
Axes of the slice: x: 2, y: 2, z: 4, core: 2. Of those that a mesh axis runs over, the one named last changes fastest.
Arguments:
- observed: float32 [4, 2, 4, 2646], P('dp', 'section', 'tensor'), may hold values from 0.25 to 8
- section_of: int32 [126], replicated, may hold values from 0 to 1, as said below
- hist_len: int32 [21], replicated, may hold values from 1 to 127
- roll_index: int32 [], replicated, may hold values from 0 to 127
- history: float32 [128, 2646], replicated, may hold values from 0.02 to 64
- acts: bfloat16 [2, 1536, 16384], P('section', 'dp', 'tensor'), may hold values from -6 to 6
- grads: bfloat16 [2, 1536, 1024], P('section', 'dp', 'tensor'), may hold values from -6 to 6
Outputs:
- new_history: float32 [128, 2646], replicated
- new_scale: float32 [2646], replicated
- wgrad: bfloat16 [2, 16384, 1024], P('section', ('tensor', 'dp'))
Inputs may be any that keep to these rules, and one draw needn't show every extreme that they name: `section_of`: layers are assigned to sections in contiguous ascending groups, and every section holds at least one layer.
All inputs are finite; a program needn't handle non-finite values.
Results may differ from a plain program's by a relative error of at most 0.017.
Values may be sent and summed in bfloat16 or wider, within the bound.
A program may use at most 64 MiB of HBM per device.

v0:
```python
import jax
import jax.numpy as jnp
from jax import lax
from jax.sharding import PartitionSpec as P

FP8_MAX = 448.0


def merge_amax(local):
    merged = lax.pmax(local, "tensor")
    merged = lax.pmax(merged, "section")
    return lax.pmax(merged, "dp")


def weight_grad(acts, grads, scale_x, scale_g):
    denom = scale_x * scale_g
    acts_q = jnp.clip(acts[0].astype(jnp.float32) * scale_x, -FP8_MAX, FP8_MAX).astype(jnp.bfloat16)
    grads_q = jnp.clip(grads[0].astype(jnp.float32) * scale_g, -FP8_MAX, FP8_MAX).astype(
        jnp.bfloat16
    )
    grads_all = lax.all_gather(grads_q, "tensor", axis=1, tiled=True)
    product = lax.dot_general(
        acts_q, grads_all, (((0,), (0,)), ((), ())), preferred_element_type=jnp.float32
    )
    summed = lax.psum_scatter(
        (product / denom).astype(jnp.bfloat16), "dp", scatter_dimension=0, tiled=True
    )
    return summed[None]


def body(observed, section_of, hist_len, roll_index, history, acts, grads):
    section = lax.axis_index("section")
    kinds = hist_len.shape[0]
    total_tensors = history.shape[1]
    slot_count = history.shape[0]
    kind_len = jnp.tile(hist_len, total_tensors // kinds)
    slots = lax.broadcasted_iota(jnp.int32, (slot_count, 1), 0)
    age = (roll_index - slots) % slot_count
    first = jnp.sum((section_of < section).astype(jnp.int32))
    columns = lax.dynamic_slice_in_dim(history, first * kinds, 2, 1)
    pair_len = hist_len[:2]
    old_window = (age >= 1) & (age <= pair_len[None, :])
    old_scale = FP8_MAX / jnp.max(jnp.where(old_window, columns, jnp.float32(0.0)), axis=0)
    owned = jnp.repeat(section_of == section, kinds)
    local = jnp.where(owned, observed.reshape(total_tensors), jnp.float32(0.0))
    merged = merge_amax(local)
    wgrad = weight_grad(acts, grads, old_scale[0], old_scale[1])
    new_history = jnp.where(slots == roll_index, merged[None, :], history)
    new_window = age < kind_len[None, :]
    new_scale = FP8_MAX / jnp.max(jnp.where(new_window, new_history, jnp.float32(0.0)), axis=0)
    return (new_history, new_scale, wgrad)


def solution(mesh):
    in_specs = (
        P("dp", "section", "tensor", None),
        P(),
        P(),
        P(),
        P(),
        P("section", "dp", "tensor"),
        P("section", "dp", "tensor"),
    )
    out_specs = (P(), P(), P("section", ("tensor", "dp"), None))
    return jax.shard_map(body, mesh=mesh, in_specs=in_specs, out_specs=out_specs, check_vma=False)
```

profile of v0, /device:TPU:0, one launch (start us, length us, event | category | flops | bytes accessed | tf_op | source)
XLA Modules:
  0.0 123.1 jit_solution(12922742336281192124)
XLA Ops:
  7.2 0.0 reduce-scatter.2.cloned.1.call-start
  7.9 1.3 %fusion.7 = s32[]{:T(128)} fusion(s32[126]{0:T(128)} %param.8, s32[]{:T(128)S(6)} %axis_index.15), kind=kLoop, calls=%fused_computation.18 | loop fusion | flops 377 | bytes 512 | tf_op jit(solution)/shard_map/reduce_sum | solution.py:39
  9.8 0.9 fusion.6
  10.7 0.6 fusion.11
  12.6 1.6 %clamp_convert_fusion.1 = bf16[1,384,256]{2,1,0:T(8,128)(2,1)S(1)} fusion(bf16[1,384,256]{2,1,0:T(8,128)(2,1)} %param.13, f32[]{:T(128)} %bitcast.2), kind=kLoop, calls=%fused_computation.9 | loop fusion | flops 393216 | bytes 393220 | tf_op jit(solution)/shard_map/convert_element_type | solution.py:18
  14.3 21.3 %all-gather = bf16[1,384,1024]{2,1,0:T(8,128)(2,1)S(1)} all-gather(bf16[1,384,256]{2,1,0:T(8,128)(2,1)S(1)} %clamp_convert_fusion.1), channel_id=2, replica_groups=mesh['dp'=4,'section'=2,'tensor'=4] {'tensor'}, dimensions={2}, use_global_device_ids=true | all-gather | bytes 983040 | tf_op jit(solution)/shard_map/all_gather | solution.py:21
  35.6 9.5 %divide_convert_fusion = bf16[4096,1024]{1,0:T(8,128)(2,1)} fusion(f32[]{:T(128)S(6)} %mul.25, bf16[1,384,4096]{2,1,0:T(8,128)(2,1)} %param.12, f32[]{:T(128)} %bitcast, bf16[1,384,1024]{2,1,0:T(8,128)(2,1)S(1)} %all-gather), kind=kOutput, calls=%fused_computation | convolution fusion | flops 3235905536 | bytes 12320776 | tf_op jit(solution)/shard_map/dot_general | solution.py:22
  45.0 0.0 copy-start.3
  45.0 0.0 copy-start.2
  45.0 0.0 copy-start.1
  45.0 0.0 reduce-scatter.2.cloned.1.call-update
  45.1 0.6 copy-done.3
  45.7 0.1 broadcast_in_dim.37
  45.8 0.2 reshape.60
  46.0 0.0 copy-done.2
  46.0 0.2 lt.30
  46.2 0.0 copy-done.1
  46.3 17.1 %pmax.21 = f32[2646]{0:T(1024)S(1)} all-reduce(f32[2646]{0:T(1024)S(1)} %broadcast_select_fusion.1), channel_id=1, replica_groups=mesh['dp'=4,'section'=2,'tensor'=4] {'tensor'}, use_global_device_ids=true, to_apply=%region_0.1 | all-reduce | flops 2646 | bytes 21168 | tf_op jit(solution)/shard_map/pmax | solution.py:10
  63.3 8.1 %pmax.22 = f32[2646]{0:T(1024)S(1)} all-reduce(f32[2646]{0:T(1024)S(1)} %pmax.21), channel_id=1, replica_groups=mesh['dp'=4,'section'=2,'tensor'=4] {'section'}, use_global_device_ids=true, to_apply=%region_1.2 | all-reduce | flops 2646 | bytes 21168 | tf_op jit(solution)/shard_map/pmax | solution.py:11
  71.4 11.8 %pmax.23 = f32[2646]{0:T(1024)S(1)} all-reduce(f32[2646]{0:T(1024)S(1)} %pmax.22), channel_id=1, replica_groups=mesh['dp'=4,'section'=2,'tensor'=4] {'dp'}, use_global_device_ids=true, to_apply=%region_2.3 | all-reduce | flops 2646 | bytes 21168 | tf_op jit(solution)/shard_map/pmax | solution.py:12
  83.2 0.0 copy-done
  83.2 2.9 %select_reduce_fusion = (f32[2646]{0:T(1024)S(1)}, f32[128,2646]{0,1:T(8,128)}) fusion(s32[128]{0:T(128)S(1)} %and_select_fusion.1, s32[2646]{0:T(1024)S(1)} %lt.30, f32[128,2646]{0,1:T(8,128)S(1)} %copy-done, f32[2646]{0:T(1024)S(1)} %pmax.23, pred[128]{0:T(512)(128)(4,1)S(1)} %iota_compare_fusion), kind=kLoop, calls=%fused_computation.6 | loop fusion | flops 1352106 | bytes 2741896 | tf_op jit(solution)/shard_map/reduce_max | solution.py:50
  86.1 0.6 broadcast_divide_fusion
  86.7 29.6 %reduce-scatter.2.cloned.1.call-done = bf16[1024,1024]{1,0:T(8,128)(2,1)} async-done(((bf16[4096,1024]{1,0:T(8,128)(2,1)}), bf16[1024,1024]{1,0:T(8,128)(2,1)}) %reduce-scatter.2.cloned.1.call-update) | async-done | bytes 2097168 | tf_op jit(solution)/shard_map/reduce_scatter | solution.py:25
  (9 shorter events, 0.1 us)
Async XLA Ops:
  7.2 109.1 %reduce-scatter.2.cloned.1.call-start = ((), (), s32[]{:S(2)}) async-start(), calls=%async_computation.1 | async-start | bytes 10485760 | tf_op jit(solution)/shard_map/reduce_scatter | solution.py:25
  45.0 0.7 copy-start.3
  45.0 1.0 copy-start.2
  45.0 1.2 copy-start.1
  45.0 38.2 %copy-start = (f32[128,2646]{0,1:T(8,128)S(1)}, f32[128,2646]{0,1:T(8,128)}, u32[]{:S(2)}) copy-start(f32[128,2646]{0,1:T(8,128)} %param.11) | copy-start | bytes 4064260
Sparse Core Ops, SparseCore 0:
  45.2 70.9 reduce-scatter.1
where the time goes:
time: 123 us
  blocking collectives  58.2 us (47%)
  waiting for transfers between devices  29.6 us (24%)
  between operations  16.7 us (14%)
  matrix products  9.46 us (8%)
  other arithmetic  7.36 us (6%)
  local copies, waits for them, and re-layouts  1.72 us (1%)
    reduce_scatter x1, waiting for transfers between devices, weight_grad(): lax.psum_scatter((product / denom).astype(jnp.bfloat16), 'dp', scatter_di...  29.6 us
    all_gather x1, blocking collectives, weight_grad(): grads_all = lax.all_gather(grads_q, 'tensor', axis=1, tiled=True)  21.3 us
    pmax x1, blocking collectives, merge_amax(): merged = lax.pmax(local, 'tensor')  17.1 us
    pmax x1, blocking collectives, merge_amax(): return lax.pmax(merged, 'dp')  11.8 us
    dot_general x1, matrix products, weight_grad(): lax.dot_general(acts_q, grads_all, (((0,), (0,)), ((), ())), preferred_el...  9.46 us
    pmax x1, blocking collectives, merge_amax(): merged = lax.pmax(merged, 'section')  8.09 us
    reduce_max x1, other arithmetic, body(): jnp.max(jnp.where(new_window, new_history, jnp.float32(0.0)), axis=0)  2.87 us
  transfers between devices with their start and end apart: 1, of which 1 were waited for; matrix products, arithmetic and copies ran while one was open for 3% of the time, Pallas kernels for 0%

commit v1 on v0

--- a/solution.py
+++ b/solution.py
@@ -18,7 +18,7 @@
     grads_q = jnp.clip(grads[0].astype(jnp.float32) * scale_g, -FP8_MAX, FP8_MAX).astype(
         jnp.bfloat16
     )
-    grads_all = lax.all_gather(grads_q, "tensor", axis=1, tiled=True)
+    grads_all = jnp.concatenate(lax.all_gather(grads_q, "tensor"), 1)
     product = lax.dot_general(
         acts_q, grads_all, (((0,), (0,)), ((), ())), preferred_element_type=jnp.float32
     )

time: 123 us -> 124 us (level)
  no operation moved by 1% of the time
where the time goes in v1:
time: 124 us; the launch traced here: 123 us
  blocking collectives  58.2 us (47%)
  waiting for transfers between devices  29.6 us (24%)
  between operations  16.7 us (13%)
  matrix products  9.48 us (8%)
  other arithmetic  7.36 us (6%)
  local copies, waits for them, and re-layouts  2.08 us (2%)
    reduce_scatter x1, waiting for transfers between devices, weight_grad(): lax.psum_scatter((product / denom).astype(jnp.bfloat16), 'dp', scatter_di...  29.6 us
    all_gather x1, blocking collectives, weight_grad(): grads_all = jnp.concatenate(lax.all_gather(grads_q, 'tensor'), 1)  21.3 us
    pmax x1, blocking collectives, merge_amax(): merged = lax.pmax(local, 'tensor')  17 us
    pmax x1, blocking collectives, merge_amax(): return lax.pmax(merged, 'dp')  11.8 us
    dot_general x1, matrix products, weight_grad(): lax.dot_general(acts_q, grads_all, (((0,), (0,)), ((), ())), preferred_el...  9.48 us
    pmax x1, blocking collectives, merge_amax(): merged = lax.pmax(merged, 'section')  8.09 us
    reduce_max x1, other arithmetic, body(): jnp.max(jnp.where(new_window, new_history, jnp.float32(0.0)), axis=0)  2.87 us
  transfers between devices with their start and end apart: 1, of which 1 were waited for; matrix products, arithmetic and copies ran while one was open for 3% of the time, Pallas kernels for 0%

profile of v1, /device:TPU:0, one launch (start us, length us, event | category | flops | bytes accessed | tf_op | source)
XLA Modules:
  0.0 123.5 jit_solution(8110476038743317213)
XLA Ops:
  7.2 0.0 reduce-scatter.2.cloned.1.call-start
  7.9 1.3 %fusion.6 = s32[]{:T(128)} fusion(s32[126]{0:T(128)} %param.8, s32[]{:T(128)S(6)} %axis_index.15), kind=kLoop, calls=%fused_computation.17 | loop fusion | flops 377 | bytes 512 | tf_op jit(solution)/shard_map/reduce_sum | solution.py:39
  9.8 0.9 fusion.5
  10.7 0.6 fusion.10
  12.6 1.6 %clamp_convert_fusion.1 = bf16[1,384,256]{2,1,0:T(8,128)(2,1)S(1)} fusion(bf16[1,384,256]{2,1,0:T(8,128)(2,1)} %param.13, f32[]{:T(128)} %bitcast.2), kind=kLoop, calls=%fused_computation.8 | loop fusion | flops 393216 | bytes 393220 | tf_op jit(solution)/shard_map/convert_element_type | solution.py:18
  14.3 21.3 %all_gather.4 = bf16[4,384,256]{2,1,0:T(8,128)(2,1)S(1)} all-gather(bf16[1,384,256]{2,1,0:T(8,128)(2,1)S(1)} %clamp_convert_fusion.1), channel_id=1, replica_groups=mesh['dp'=4,'section'=2,'tensor'=4] {'tensor'}, dimensions={0}, use_global_device_ids=true | all-gather | bytes 983040 | tf_op jit(solution)/shard_map/all_gather | solution.py:21
  35.6 0.4 copy.11
  35.9 9.5 %divide_convert_fusion = bf16[4096,1024]{1,0:T(8,128)(2,1)} fusion(f32[]{:T(128)S(6)} %mul.25, bf16[384,1024]{0,1:T(8,128)(2,1)S(1)} %bitcast.11, bf16[1,384,4096]{2,1,0:T(8,128)(2,1)} %param.12, f32[]{:T(128)} %bitcast), kind=kOutput, calls=%fused_computation | convolution fusion | flops 3235905536 | bytes 12320776 | tf_op jit(solution)/shard_map/dot_general | solution.py:22
  45.4 0.0 copy-start.3
  45.4 0.0 copy-start.1
  45.4 0.0 reduce-scatter.2.cloned.1.call-update
  45.4 0.6 copy-done.3
  46.1 0.1 broadcast_in_dim.37
  46.2 0.2 reshape.53
  46.4 0.0 copy-done.2
  46.4 0.2 lt.30
  46.6 0.0 copy-done.1
  46.7 17.0 %pmax.21 = f32[2646]{0:T(1024)S(1)} all-reduce(f32[2646]{0:T(1024)S(1)} %broadcast_select_fusion.1), channel_id=1, replica_groups=mesh['dp'=4,'section'=2,'tensor'=4] {'tensor'}, use_global_device_ids=true, to_apply=%region_0.1 | all-reduce | flops 2646 | bytes 21168 | tf_op jit(solution)/shard_map/pmax | solution.py:10
  63.7 8.1 %pmax.22 = f32[2646]{0:T(1024)S(1)} all-reduce(f32[2646]{0:T(1024)S(1)} %pmax.21), channel_id=1, replica_groups=mesh['dp'=4,'section'=2,'tensor'=4] {'section'}, use_global_device_ids=true, to_apply=%region_1.2 | all-reduce | flops 2646 | bytes 21168 | tf_op jit(solution)/shard_map/pmax | solution.py:11
  71.8 11.8 %pmax.23 = f32[2646]{0:T(1024)S(1)} all-reduce(f32[2646]{0:T(1024)S(1)} %pmax.22), channel_id=1, replica_groups=mesh['dp'=4,'section'=2,'tensor'=4] {'dp'}, use_global_device_ids=true, to_apply=%region_2.3 | all-reduce | flops 2646 | bytes 21168 | tf_op jit(solution)/shard_map/pmax | solution.py:12
  83.6 0.0 copy-done
  83.6 2.9 %select_reduce_fusion = (f32[2646]{0:T(1024)S(1)}, f32[128,2646]{0,1:T(8,128)}) fusion(s32[128]{0:T(128)S(1)} %and_select_fusion.1, s32[2646]{0:T(1024)S(1)} %lt.30, f32[128,2646]{0,1:T(8,128)S(1)} %copy-done, f32[2646]{0:T(1024)S(1)} %pmax.23, pred[128]{0:T(512)(128)(4,1)S(1)} %iota_compare_fusion), kind=kLoop, calls=%fused_computation.6 | loop fusion | flops 1352106 | bytes 2741896 | tf_op jit(solution)/shard_map/reduce_max | solution.py:50
  86.4 0.6 broadcast_divide_fusion
  87.1 29.6 %reduce-scatter.2.cloned.1.call-done = bf16[1024,1024]{1,0:T(8,128)(2,1)} async-done(((bf16[4096,1024]{1,0:T(8,128)(2,1)}), bf16[1024,1024]{1,0:T(8,128)(2,1)}) %reduce-scatter.2.cloned.1.call-update) | async-done | bytes 2097168 | tf_op jit(solution)/shard_map/reduce_scatter | solution.py:25
  (10 shorter events, 0.1 us)
Async XLA Ops:
  7.2 109.4 %reduce-scatter.2.cloned.1.call-start = ((), (), s32[]{:S(2)}) async-start(), calls=%async_computation.1 | async-start | bytes 10485760 | tf_op jit(solution)/shard_map/reduce_scatter | solution.py:25
  45.4 0.7 copy-start.3
  45.4 1.0 copy-start.2
  45.4 1.2 copy-start.1
  45.4 38.2 %copy-start = (f32[128,2646]{0,1:T(8,128)S(1)}, f32[128,2646]{0,1:T(8,128)}, u32[]{:S(2)}) copy-start(f32[128,2646]{0,1:T(8,128)} %param.11) | copy-start | bytes 4064260
Sparse Core Ops, SparseCore 0:
  45.6 70.9 reduce-scatter.1
